TPU v7x, 32 devices: a whole 2x2x4 slice. The times are simulated.
32 devices in a mesh: group: 4 (over y, core), sub: 8 (over z, x).
Axes of the slice: x: 2, y: 2, z: 4, core: 2. Of those that a mesh axis runs over, the one named last changes fastest.
Arguments:
- shared_sizes: int32 [4, 8, 2], P('group', 'sub'), may hold values from 0 to 256, as said below
- stiffness: float32 [4, 8], P('group', 'sub'), may hold values from 0.1 to 10
- load_cases: float32 [4, 8, 1024, 384], P('group', 'sub'), may hold values from -6 to 6
- schur_blocks: bfloat16 [4, 8, 1024, 1024], P('group', 'sub')
- neumann_inverse: bfloat16 [4, 8, 1024, 1024], P('group', 'sub')
- coarse_basis: bfloat16 [4, 8, 32, 1024], P('group', 'sub'), may hold values from -0.1875 to 0.1875
- coarse_dofs: int32 [4, 8, 32], P('group', 'sub'), may hold values from 0 to 511
- coarse_inverse: float32 [512, 512], P('sub'), as said below
Outputs:
- solution: float32 [4, 8, 1024, 384], P('group', 'sub')
- residual: float32 [4, 8, 1024, 384], P('group', 'sub')
Inputs may be any that keep to these rules, and one draw needn't show every extreme that they name: shared_sizes[g, s, 0] equals shared_sizes[g, s - 1, 1]; the lower share of the first and the upper share of the last subdomain of a group are 0, the other shares lie in 128 to 256, and in every group some subdomain shares exactly 256 with its upper neighbour. `coarse_inverse`: symmetric.
All inputs are finite; a program needn't handle non-finite values.
Results may differ from a plain program's by a relative error of at most 0.0075.
Values sent between devices are 32-bit elements; how exact they have to be, the bound alone decides.
No kernel may reach another device: no remote copies, remote signals or barrier semaphores. Data moves between devices by JAX's collectives and lax.ppermute only.
A program may use at most 128 MiB of HBM per device.

v0:
```python
import jax
import jax.numpy as jnp
from jax import lax
from jax.sharding import PartitionSpec as P

MAXSH = 256
ITERS = 4
OMEGA = 0.6


def from_behind(block, axis, distance):
    devices = range(lax.axis_size(axis))
    route = [(i - distance, i) for i in devices if i - distance in devices]
    return lax.ppermute(block, axis, route)


def extended(x, sides, width):
    for axis, dim in sides:
        peers, length = (lax.axis_size(axis), x.shape[dim])
        up = [(i, (i + 1) % peers) for i in range(peers - 1)]
        down = [(j, i) for i, j in up]
        last = lax.slice_in_dim(x, length - width, length, axis=dim)
        leading = lax.slice_in_dim(x, 0, width, axis=dim)
        before = lax.ppermute(last, axis, up)
        after = lax.ppermute(leading, axis, down)
        x = jnp.concatenate([before, x, after], axis=dim)
    return x


def lift_piece(tail_rows, share_size):
    slab_width = tail_rows.shape[0]
    rolled = jnp.roll(tail_rows, share_size - slab_width, axis=0)
    inside = (jnp.arange(slab_width) < share_size)[:, None]
    return jnp.where(inside, rolled, jnp.zeros_like(rolled))


def place_piece(head_rows, share_size):
    slab_width = head_rows.shape[0]
    inside = (jnp.arange(slab_width) < share_size)[:, None]
    masked = jnp.where(inside, head_rows, jnp.zeros_like(head_rows))
    return jnp.roll(masked, slab_width - share_size, axis=0)


def assemble(vector, share_up):
    unknowns = vector.shape[0]
    tail_rows = vector[unknowns - MAXSH :]
    head_rows = vector[:MAXSH]
    lifted = lift_piece(tail_rows, share_up)
    from_lower = from_behind(lifted, "sub", 1)
    from_upper = from_behind(head_rows, "sub", -1)
    placed = place_piece(from_upper, share_up)
    return jnp.concatenate(
        [head_rows + from_lower, vector[MAXSH : unknowns - MAXSH], tail_rows + placed], axis=0
    )


def on_device(
    shared_sizes,
    stiffness,
    load_cases,
    schur_blocks,
    neumann_inverse,
    coarse_basis,
    coarse_dofs,
    coarse_inverse,
):
    share_low = shared_sizes[0, 0, 0]
    share_up = shared_sizes[0, 0, 1]
    beside_all = extended(stiffness, (("sub", 1),), 1)
    own_stiff = beside_all[0, 1]
    low_weight = own_stiff / (own_stiff + beside_all[0, 0])
    up_weight = own_stiff / (own_stiff + beside_all[0, 2])
    loads = load_cases[0, 0]
    schur = schur_blocks[0, 0]
    neumann = neumann_inverse[0, 0]
    basis = coarse_basis[0, 0]
    my_dofs = coarse_dofs[0, 0]
    unknowns, cases = loads.shape
    own_count = coarse_inverse.shape[0]
    row_index = jnp.arange(unknowns)
    weight = jnp.where(
        row_index < share_low,
        low_weight,
        jnp.where(row_index >= unknowns - share_up, up_weight, jnp.float32(1.0)),
    )[:, None]
    highest = lax.Precision.HIGHEST

    def operator_residual(solution):
        return loads - jnp.dot(
            schur, solution.astype(jnp.bfloat16), preferred_element_type=jnp.float32
        )

    solution = jnp.zeros((unknowns, cases), jnp.float32)
    for sweep in range(ITERS):
        local = operator_residual(solution)
        weighted = (weight * assemble(local, share_up)).astype(jnp.bfloat16)
        coarse_terms = jnp.dot(basis, weighted, preferred_element_type=jnp.float32)
        dof_values = my_dofs.astype(jnp.float32)
        all_terms = lax.all_gather(coarse_terms, "sub", axis=0, tiled=True)
        all_dofs = lax.all_gather(dof_values, "sub", axis=0, tiled=True)
        dof_index = all_dofs.astype(jnp.int32)
        first_row = lax.axis_index("sub") * own_count
        own_select = (dof_index[:, None] == first_row + jnp.arange(own_count)[None, :]).astype(
            jnp.float32
        )
        owned = lax.dot_general(own_select, all_terms, (((0,), (0,)), ((), ())), precision=highest)
        owned = lax.psum(owned, "group")
        columns = jnp.take(coarse_inverse, dof_index, axis=1)
        partial_vals = lax.dot_general(columns, owned, (((0,), (0,)), ((), ())), precision=highest)
        partial_vals = partial_vals.reshape(-1, coarse_terms.shape[0], cases)
        received = lax.all_to_all(partial_vals, "sub", split_axis=0, concat_axis=0, tiled=True)
        picked = jnp.sum(received, axis=0)
        picked = picked.astype(jnp.bfloat16)
        correction = jnp.dot(neumann, weighted, preferred_element_type=jnp.float32)
        correction = correction + lax.dot_general(
            basis, picked, (((0,), (0,)), ((), ())), preferred_element_type=jnp.float32
        )
        solution = solution + OMEGA * assemble(weight * correction, share_up)
    residual = assemble(operator_residual(solution), share_up)
    return (solution[None, None], residual[None, None])


def solution(mesh):
    return jax.shard_map(
        on_device,
        mesh=mesh,
        in_specs=(
            P("group", "sub", None),
            P("group", "sub"),
            P("group", "sub", None, None),
            P("group", "sub", None, None),
            P("group", "sub", None, None),
            P("group", "sub", None, None),
            P("group", "sub", None),
            P("sub", None),
        ),
        out_specs=(P("group", "sub", None, None), P("group", "sub", None, None)),
        check_vma=False,
    )
```

profile of v0, /device:TPU:16, one launch (start us, length us, event | category | flops | bytes accessed | tf_op | source)
XLA Modules:
  0.0 597.5 jit_solution(9661922671992732006)
XLA Ops:
  7.2 3.4 collective-permute-start.1
  10.7 2.6 collective-permute-start
  13.2 3.0 copy.14
  16.2 2.4 bitcast_subtract_fusion.4
  20.8 4.2 collective-permute-start.3
  31.0 14.9 %all-reduce = f32[256]{0:T(256)S(1)} all-reduce(f32[256]{0:T(256)S(1)} %bitcast_dynamic-update-slice_fusion), channel_id=2, replica_groups=mesh['group'=4,'sub'=8] {'sub'}, use_global_device_ids=true, to_apply=%add | all-reduce | flops 256 | bytes 2048
  47.3 2.2 fusion.89
  49.6 2.8 collective-permute-start.2
  54.6 6.0 %collective-permute-done.2 = f32[256,384]{0,1:T(8,128)} collective-permute-done((f32[256,384]{0,1:T(8,128)}, f32[256,384]{0,1:T(8,128)}, u32[]{:S(2)}, u32[]{:S(2)}) %collective-permute-start.2) | collective-permute-done | bytes 393248 | tf_op jit(solution)/shard_map/ppermute | solution.py:14
  60.6 1.5 slice_add_fusion.8
  63.2 27.9 %all_gather.19 = f32[256,384]{1,0:T(8,128)S(1)} all-gather(f32[32,384]{1,0:T(8,128)S(1)} %convolution_bitcast_fusion.3), channel_id=1, replica_groups=mesh['group'=4,'sub'=8] {'sub'}, dimensions={0}, use_global_device_ids=true | all-gather | bytes 442368 | tf_op jit(solution)/shard_map/all_gather | solution.py:99
  93.1 34.8 %all-reduce.6.cloned.1.call-done = f32[64,384]{1,0:T(8,128)} async-done(((f32[64,384]{1,0:T(8,128)}), f32[64,384]{1,0:T(8,128)}) %all-reduce.6.cloned.1.call-update) | async-done | bytes 98320 | tf_op jit(solution)/shard_map/psum | solution.py:107
  127.9 1.4 fusion.107
  129.4 15.0 %all_to_all.20 = f32[8,32,384]{2,1,0:T(8,128)} all-to-all(f32[8,32,384]{2,1,0:T(8,128)S(1)} %bitcast.145), channel_id=1, replica_groups=mesh['group'=4,'sub'=8] {'sub'}, dimensions={0} | all-to-all | bytes 786432 | tf_op jit(solution)/shard_map/all_to_all | solution.py:111
  146.4 2.6 multiply_bitcast_fusion.3
  149.1 3.2 collective-permute-start.5
  152.3 8.6 %collective-permute-done.5 = f32[256,384]{0,1:T(8,128)S(1)} collective-permute-done((f32[256,384]{0,1:T(8,128)S(1)}, f32[256,384]{0,1:T(8,128)S(1)}, u32[]{:S(2)}, u32[]{:S(2)}) %collective-permute-start.5) | collective-permute-done | bytes 393248 | tf_op jit(solution)/shard_map/ppermute | solution.py:14
  161.2 3.0 collective-permute-start.4
  165.2 7.9 %collective-permute-done.4 = f32[256,384]{0,1:T(8,128)S(1)} collective-permute-done((f32[256,384]{0,1:T(8,128)S(1)}, f32[256,384]{0,1:T(8,128)S(1)}, u32[]{:S(2)}, u32[]{:S(2)}) %collective-permute-start.4) | collective-permute-done | bytes 393248 | tf_op jit(solution)/shard_map/ppermute | solution.py:14
  174.6 1.9 collective-permute-start.7
  176.5 8.2 %collective-permute-done.7 = f32[256,384]{0,1:T(8,128)S(1)} collective-permute-done((f32[256,384]{0,1:T(8,128)S(1)}, f32[256,384]{0,1:T(8,128)S(1)}, u32[]{:S(2)}, u32[]{:S(2)}) %collective-permute-start.7) | collective-permute-done | bytes 393248 | tf_op jit(solution)/shard_map/ppermute | solution.py:14
  185.0 2.5 collective-permute-start.6
  187.6 8.1 %collective-permute-done.6 = f32[256,384]{0,1:T(8,128)S(1)} collective-permute-done((f32[256,384]{0,1:T(8,128)S(1)}, f32[256,384]{0,1:T(8,128)S(1)}, u32[]{:S(2)}, u32[]{:S(2)}) %collective-permute-start.6) | collective-permute-done | bytes 393248 | tf_op jit(solution)/shard_map/ppermute | solution.py:14
  196.3 25.4 %all_gather.20 = f32[256,384]{1,0:T(8,128)S(1)} all-gather(f32[32,384]{1,0:T(8,128)S(1)} %convolution_bitcast_fusion.2), channel_id=1, replica_groups=mesh['group'=4,'sub'=8] {'sub'}, dimensions={0}, use_global_device_ids=true | all-gather | bytes 442368 | tf_op jit(solution)/shard_map/all_gather | solution.py:99
  222.8 34.4 %all-reduce.8.cloned.1.call-done = f32[64,384]{1,0:T(8,128)} async-done(((f32[64,384]{1,0:T(8,128)}), f32[64,384]{1,0:T(8,128)}) %all-reduce.8.cloned.1.call-update) | async-done | bytes 98320 | tf_op jit(solution)/shard_map/psum | solution.py:107
  257.2 1.4 fusion.105
  258.6 14.9 %all_to_all.21 = f32[8,32,384]{2,1,0:T(8,128)} all-to-all(f32[8,32,384]{2,1,0:T(8,128)S(1)} %bitcast.146), channel_id=1, replica_groups=mesh['group'=4,'sub'=8] {'sub'}, dimensions={0} | all-to-all | bytes 786432 | tf_op jit(solution)/shard_map/all_to_all | solution.py:111
  275.7 2.6 multiply_bitcast_fusion.2
  278.5 3.2 collective-permute-start.9
  281.7 8.6 %collective-permute-done.9 = f32[256,384]{0,1:T(8,128)S(1)} collective-permute-done((f32[256,384]{0,1:T(8,128)S(1)}, f32[256,384]{0,1:T(8,128)S(1)}, u32[]{:S(2)}, u32[]{:S(2)}) %collective-permute-start.9) | collective-permute-done | bytes 393248 | tf_op jit(solution)/shard_map/ppermute | solution.py:14
  290.6 3.2 collective-permute-start.8
  294.9 7.6 %collective-permute-done.8 = f32[256,384]{0,1:T(8,128)S(1)} collective-permute-done((f32[256,384]{0,1:T(8,128)S(1)}, f32[256,384]{0,1:T(8,128)S(1)}, u32[]{:S(2)}, u32[]{:S(2)}) %collective-permute-start.8) | collective-permute-done | bytes 393248 | tf_op jit(solution)/shard_map/ppermute | solution.py:14
  303.9 1.9 collective-permute-start.11
  305.9 8.2 %collective-permute-done.11 = f32[256,384]{0,1:T(8,128)S(1)} collective-permute-done((f32[256,384]{0,1:T(8,128)S(1)}, f32[256,384]{0,1:T(8,128)S(1)}, u32[]{:S(2)}, u32[]{:S(2)}) %collective-permute-start.11) | collective-permute-done | bytes 393248 | tf_op jit(solution)/shard_map/ppermute | solution.py:14
  314.3 2.6 collective-permute-start.10
  317.0 8.0 %collective-permute-done.10 = f32[256,384]{0,1:T(8,128)S(1)} collective-permute-done((f32[256,384]{0,1:T(8,128)S(1)}, f32[256,384]{0,1:T(8,128)S(1)}, u32[]{:S(2)}, u32[]{:S(2)}) %collective-permute-start.10) | collective-permute-done | bytes 393248 | tf_op jit(solution)/shard_map/ppermute | solution.py:14
  325.7 25.4 %all_gather.21 = f32[256,384]{1,0:T(8,128)S(1)} all-gather(f32[32,384]{1,0:T(8,128)S(1)} %convolution_bitcast_fusion.1), channel_id=1, replica_groups=mesh['group'=4,'sub'=8] {'sub'}, dimensions={0}, use_global_device_ids=true | all-gather | bytes 442368 | tf_op jit(solution)/shard_map/all_gather | solution.py:99
  352.2 34.4 %all-reduce.10.cloned.1.call-done = f32[64,384]{1,0:T(8,128)} async-done(((f32[64,384]{1,0:T(8,128)}), f32[64,384]{1,0:T(8,128)}) %all-reduce.10.cloned.1.call-update) | async-done | bytes 98320 | tf_op jit(solution)/shard_map/psum | solution.py:107
  388.0 14.9 %all_to_all.22 = f32[8,32,384]{2,1,0:T(8,128)} all-to-all(f32[8,32,384]{2,1,0:T(8,128)S(1)} %bitcast.147), channel_id=1, replica_groups=mesh['group'=4,'sub'=8] {'sub'}, dimensions={0} | all-to-all | bytes 786432 | tf_op jit(solution)/shard_map/all_to_all | solution.py:111
  405.1 2.7 multiply_bitcast_fusion.1
  407.9 3.2 collective-permute-start.13
  411.1 8.6 %collective-permute-done.13 = f32[256,384]{0,1:T(8,128)S(1)} collective-permute-done((f32[256,384]{0,1:T(8,128)S(1)}, f32[256,384]{0,1:T(8,128)S(1)}, u32[]{:S(2)}, u32[]{:S(2)}) %collective-permute-start.13) | collective-permute-done | bytes 393248 | tf_op jit(solution)/shard_map/ppermute | solution.py:14
  420.0 3.0 collective-permute-start.12
  424.0 7.9 %collective-permute-done.12 = f32[256,384]{0,1:T(8,128)S(1)} collective-permute-done((f32[256,384]{0,1:T(8,128)S(1)}, f32[256,384]{0,1:T(8,128)S(1)}, u32[]{:S(2)}, u32[]{:S(2)}) %collective-permute-start.12) | collective-permute-done | bytes 393248 | tf_op jit(solution)/shard_map/ppermute | solution.py:14
  433.4 1.9 collective-permute-start.15
  435.4 8.2 %collective-permute-done.15 = f32[256,384]{0,1:T(8,128)S(1)} collective-permute-done((f32[256,384]{0,1:T(8,128)S(1)}, f32[256,384]{0,1:T(8,128)S(1)}, u32[]{:S(2)}, u32[]{:S(2)}) %collective-permute-start.15) | collective-permute-done | bytes 393248 | tf_op jit(solution)/shard_map/ppermute | solution.py:14
  443.9 2.5 collective-permute-start.14
  446.5 8.1 %collective-permute-done.14 = f32[256,384]{0,1:T(8,128)S(1)} collective-permute-done((f32[256,384]{0,1:T(8,128)S(1)}, f32[256,384]{0,1:T(8,128)S(1)}, u32[]{:S(2)}, u32[]{:S(2)}) %collective-permute-start.14) | collective-permute-done | bytes 393248 | tf_op jit(solution)/shard_map/ppermute | solution.py:14
  455.2 25.4 %all_gather.22 = f32[256,384]{1,0:T(8,128)S(1)} all-gather(f32[32,384]{1,0:T(8,128)S(1)} %convolution_bitcast_fusion), channel_id=1, replica_groups=mesh['group'=4,'sub'=8] {'sub'}, dimensions={0}, use_global_device_ids=true | all-gather | bytes 442368 | tf_op jit(solution)/shard_map/all_gather | solution.py:99
  481.6 34.4 %all-reduce.12.cloned.1.call-done = f32[64,384]{1,0:T(8,128)} async-done(((f32[64,384]{1,0:T(8,128)}), f32[64,384]{1,0:T(8,128)}) %all-reduce.12.cloned.1.call-update) | async-done | bytes 98320 | tf_op jit(solution)/shard_map/psum | solution.py:107
  517.5 14.9 %all_to_all.23 = f32[8,32,384]{2,1,0:T(8,128)} all-to-all(f32[8,32,384]{2,1,0:T(8,128)S(1)} %bitcast.144), channel_id=1, replica_groups=mesh['group'=4,'sub'=8] {'sub'}, dimensions={0} | all-to-all | bytes 786432 | tf_op jit(solution)/shard_map/all_to_all | solution.py:111
  534.6 2.7 multiply_bitcast_fusion
  537.3 3.2 collective-permute-start.17
  540.6 8.6 %collective-permute-done.17 = f32[256,384]{0,1:T(8,128)S(1)} collective-permute-done((f32[256,384]{0,1:T(8,128)S(1)}, f32[256,384]{0,1:T(8,128)S(1)}, u32[]{:S(2)}, u32[]{:S(2)}) %collective-permute-start.17) | collective-permute-done | bytes 393248 | tf_op jit(solution)/shard_map/ppermute | solution.py:14
  549.5 3.0 collective-permute-start.16
  552.6 8.7 %collective-permute-done.16 = f32[256,384]{0,1:T(8,128)S(1)} collective-permute-done((f32[256,384]{0,1:T(8,128)S(1)}, f32[256,384]{0,1:T(8,128)S(1)}, u32[]{:S(2)}, u32[]{:S(2)}) %collective-permute-start.16) | collective-permute-done | bytes 393248 | tf_op jit(solution)/shard_map/ppermute | solution.py:14
  563.1 1.9 collective-permute-start.19
  565.0 8.2 %collective-permute-done.19 = f32[256,384]{0,1:T(8,128)S(1)} collective-permute-done((f32[256,384]{0,1:T(8,128)S(1)}, f32[256,384]{0,1:T(8,128)S(1)}, u32[]{:S(2)}, u32[]{:S(2)}) %collective-permute-start.19) | collective-permute-done | bytes 393248 | tf_op jit(solution)/shard_map/ppermute | solution.py:14
  574.3 2.5 collective-permute-start.18
  576.8 1.7 fusion.21
  578.5 3.0 copy.16
  581.5 3.6 collective-permute-done.18
  585.1 1.5 slice_add_fusion
  588.0 3.0 copy.17
  (183 shorter events, 40.4 us)
Async XLA Ops:
  7.2 9.1 %copy-start = (bf16[1,1,1024,1024]{3,2,1,0:T(8,128)(2,1)S(1)}, bf16[1,1,1024,1024]{3,2,1,0:T(8,128)(2,1)}, u32[]{:S(2)}) copy-start(bf16[1,1,1024,1024]{3,2,1,0:T(8,128)(2,1)} %param.15) | copy-start | bytes 6291460
  7.2 120.8 %all-reduce.6.cloned.1.call-start = ((), (), s32[]{:S(2)}) async-start(), calls=%async_computation.4 | async-start | bytes 196608 | tf_op jit(solution)/shard_map/psum | solution.py:107
  7.2 45.2 %collective-permute-start.1 = (f32[1,1]{1,0:T(1,128)}, f32[1,1]{1,0:T(1,128)}, u32[]{:S(2)}, u32[]{:S(2)}) collective-permute-start(f32[1,1]{1,0:T(1,128)} %param.13), channel_id=1, source_target_pairs={{1,0},{2,1},{3,2},{4,3},{5,4},{6,5},{7,6},{9,8},{10,9},{11,10},{12... | collective-permute-start | bytes 20 | tf_op jit(solution)/shard_map/ppermute | solution.py:25
  10.7 42.5 %collective-permute-start = (f32[1,1]{1,0:T(1,128)}, f32[1,1]{1,0:T(1,128)}, u32[]{:S(2)}, u32[]{:S(2)}) collective-permute-start(f32[1,1]{1,0:T(1,128)} %param.13), channel_id=1, source_target_pairs={{0,1},{1,2},{2,3},{3,4},{4,5},{5,6},{6,7},{8,9},{9,10},{10,11},{11... | collective-permute-start | bytes 20 | tf_op jit(solution)/shard_map/ppermute | solution.py:24
  19.8 5.2 copy-start.50
  19.8 6.5 %copy-start.49 = (s32[1,1,32]{2,1,0:T(1,128)S(1)}, s32[1,1,32]{2,1,0:T(1,128)}, u32[]{:S(2)}) copy-start(s32[1,1,32]{2,1,0:T(1,128)} %param.18) | copy-start | bytes 388
  19.8 6.6 %copy-start.48 = (s32[1,1,2]{2,1,0:T(1,128)S(1)}, s32[1,1,2]{2,1,0:T(1,128)}, u32[]{:S(2)}) copy-start(s32[1,1,2]{2,1,0:T(1,128)} %param.12) | copy-start | bytes 28
  20.8 25.8 %collective-permute-start.3 = (f32[256,384]{0,1:T(8,128)}, f32[256,384]{0,1:T(8,128)S(1)}, u32[]{:S(2)}, u32[]{:S(2)}) collective-permute-start(f32[256,384]{0,1:T(8,128)} %get-tuple-element.51), channel_id=1, source_target_pairs={{1,0},{2,1},{3,2},{4,3},{5,4},{6,5},{7,6},{9,8},{10,9},{11,10},{12... | collective-permute-start | bytes 1179656 | tf_op jit(solution)/shard_map/ppermute | solution.py:14
  49.6 13.3 %copy-start.40 = (bf16[1,1,32,1024]{3,2,1,0:T(8,128)(2,1)S(1)}, bf16[1,1,32,1024]{3,2,1,0:T(8,128)(2,1)}, u32[]{:S(2)}) copy-start(bf16[1,1,32,1024]{3,2,1,0:T(8,128)(2,1)} %param.17) | copy-start | bytes 196612
  49.6 11.0 %collective-permute-start.2 = (f32[256,384]{0,1:T(8,128)}, f32[256,384]{0,1:T(8,128)}, u32[]{:S(2)}, u32[]{:S(2)}) collective-permute-start(f32[256,384]{0,1:T(8,128)} %get-tuple-element.70), channel_id=1, source_target_pairs={{0,1},{1,2},{2,3},{3,4},{4,5},{5,6},{6,7},{8,9},{9,10},{10,11},{11... | collective-permute-start | bytes 1179656 | tf_op jit(solution)/shard_map/ppermute | solution.py:14
  62.8 29.4 %copy-start.47 = (f32[64,512]{1,0:T(8,128)S(1)}, f32[64,512]{1,0:T(8,128)}, u32[]{:S(2)}) copy-start(f32[64,512]{1,0:T(8,128)} %param.19) | copy-start | bytes 393220
  92.2 165.0 %all-reduce.8.cloned.1.call-start = ((), (), s32[]{:S(2)}) async-start(), calls=%async_computation.5 | async-start | bytes 196608 | tf_op jit(solution)/shard_map/psum | solution.py:107
  129.4 16.4 %copy-start.21 = (f32[256,384]{0,1:T(8,128)S(1)}, f32[256,384]{0,1:T(8,128)}, u32[]{:S(2)}) copy-start(f32[256,384]{0,1:T(8,128)} %copy-done.20) | copy-start | bytes 1179652
  149.1 11.8 %collective-permute-start.5 = (f32[256,384]{0,1:T(8,128)S(1)}, f32[256,384]{0,1:T(8,128)S(1)}, u32[]{:S(2)}, u32[]{:S(2)}) collective-permute-start(f32[256,384]{0,1:T(8,128)S(1)} %get-tuple-element.47), channel_id=1, source_target_pairs={{1,0},{2,1},{3,2},{4,3},{5,4},{6,5},{7,6},{9,8},{10,9},{11,10},{12... | collective-permute-start | bytes 1179656 | tf_op jit(solution)/shard_map/ppermute | solution.py:14
  161.2 11.9 %collective-permute-start.4 = (f32[256,384]{0,1:T(8,128)S(1)}, f32[256,384]{0,1:T(8,128)S(1)}, u32[]{:S(2)}, u32[]{:S(2)}) collective-permute-start(f32[256,384]{0,1:T(8,128)S(1)} %get-tuple-element.66), channel_id=1, source_target_pairs={{0,1},{1,2},{2,3},{3,4},{4,5},{5,6},{6,7},{8,9},{9,10},{10,11},{11... | collective-permute-start | bytes 1179656 | tf_op jit(solution)/shard_map/ppermute | solution.py:14
  165.2 9.3 %copy-start.13 = (f32[512,384]{0,1:T(8,128)}, f32[512,384]{0,1:T(8,128)S(1)}, u32[]{:S(2)}) copy-start(f32[512,384]{0,1:T(8,128)S(1)} %get-tuple-element.42) | copy-start | bytes 2359300
  165.2 8.2 %copy-start.1 = (f32[1,1,1024,384]{2,3,1,0:T(8,128)S(1)}, f32[1,1,1024,384]{2,3,1,0:T(8,128)}, u32[]{:S(2)}) copy-start(f32[1,1,1024,384]{2,3,1,0:T(8,128)} %copy.14) | copy-start | bytes 4718596
  174.6 10.1 %collective-permute-start.7 = (f32[256,384]{0,1:T(8,128)S(1)}, f32[256,384]{0,1:T(8,128)S(1)}, u32[]{:S(2)}, u32[]{:S(2)}) collective-permute-start(f32[256,384]{0,1:T(8,128)S(1)} %get-tuple-element.41), channel_id=1, source_target_pairs={{1,0},{2,1},{3,2},{4,3},{5,4},{6,5},{7,6},{9,8},{10,9},{11,10},{12... | collective-permute-start | bytes 1179656 | tf_op jit(solution)/shard_map/ppermute | solution.py:14
  185.0 10.7 %collective-permute-start.6 = (f32[256,384]{0,1:T(8,128)S(1)}, f32[256,384]{0,1:T(8,128)S(1)}, u32[]{:S(2)}, u32[]{:S(2)}) collective-permute-start(f32[256,384]{0,1:T(8,128)S(1)} %get-tuple-element.64), channel_id=1, source_target_pairs={{0,1},{1,2},{2,3},{3,4},{4,5},{5,6},{6,7},{8,9},{9,10},{10,11},{11... | collective-permute-start | bytes 1179656 | tf_op jit(solution)/shard_map/ppermute | solution.py:14
  187.6 8.7 %copy-start.9 = (f32[512,384]{0,1:T(8,128)}, f32[512,384]{0,1:T(8,128)S(1)}, u32[]{:S(2)}) copy-start(f32[512,384]{0,1:T(8,128)S(1)} %slice.126) | copy-start | bytes 2359300
  195.9 25.8 %copy-start.26 = (f32[256,384]{0,1:T(8,128)}, f32[256,384]{0,1:T(8,128)S(1)}, u32[]{:S(2)}) copy-start(f32[256,384]{0,1:T(8,128)S(1)} %get-tuple-element.39) | copy-start | bytes 1179652
  222.7 163.8 %all-reduce.10.cloned.1.call-start = ((), (), s32[]{:S(2)}) async-start(), calls=%async_computation.6 | async-start | bytes 196608 | tf_op jit(solution)/shard_map/psum | solution.py:107
  274.5 1.2 copy-start.27
  278.5 11.8 %collective-permute-start.9 = (f32[256,384]{0,1:T(8,128)S(1)}, f32[256,384]{0,1:T(8,128)S(1)}, u32[]{:S(2)}, u32[]{:S(2)}) collective-permute-start(f32[256,384]{0,1:T(8,128)S(1)} %get-tuple-element.37), channel_id=1, source_target_pairs={{1,0},{2,1},{3,2},{4,3},{5,4},{6,5},{7,6},{9,8},{10,9},{11,10},{12... | collective-permute-start | bytes 1179656 | tf_op jit(solution)/shard_map/ppermute | solution.py:14
  290.6 11.9 %collective-permute-start.8 = (f32[256,384]{0,1:T(8,128)S(1)}, f32[256,384]{0,1:T(8,128)S(1)}, u32[]{:S(2)}, u32[]{:S(2)}) collective-permute-start(f32[256,384]{0,1:T(8,128)S(1)} %get-tuple-element.62), channel_id=1, source_target_pairs={{0,1},{1,2},{2,3},{3,4},{4,5},{5,6},{6,7},{8,9},{9,10},{10,11},{11... | collective-permute-start | bytes 1179656 | tf_op jit(solution)/shard_map/ppermute | solution.py:14
  294.9 9.0 %copy-start.41 = (f32[512,384]{0,1:T(8,128)}, f32[512,384]{0,1:T(8,128)S(1)}, u32[]{:S(2)}) copy-start(f32[512,384]{0,1:T(8,128)S(1)} %get-tuple-element.32) | copy-start | bytes 2359300
  294.9 7.9 %copy-start.2 = (f32[1,1,1024,384]{2,3,1,0:T(8,128)S(1)}, f32[1,1,1024,384]{2,3,1,0:T(8,128)}, u32[]{:S(2)}) copy-start(f32[1,1,1024,384]{2,3,1,0:T(8,128)} %copy.14) | copy-start | bytes 4718596
  294.9 7.9 %copy-start.14 = (f32[512,384]{0,1:T(8,128)S(1)}, f32[512,384]{0,1:T(8,128)}, u32[]{:S(2)}) copy-start(f32[512,384]{0,1:T(8,128)} %copy-done.13) | copy-start | bytes 2359300
  303.9 10.1 %collective-permute-start.11 = (f32[256,384]{0,1:T(8,128)S(1)}, f32[256,384]{0,1:T(8,128)S(1)}, u32[]{:S(2)}, u32[]{:S(2)}) collective-permute-start(f32[256,384]{0,1:T(8,128)S(1)} %get-tuple-element.31), channel_id=1, source_target_pairs={{1,0},{2,1},{3,2},{4,3},{5,4},{6,5},{7,6},{9,8},{10,9},{11,10},{12... | collective-permute-start | bytes 1179656 | tf_op jit(solution)/shard_map/ppermute | solution.py:14
  314.3 10.7 %collective-permute-start.10 = (f32[256,384]{0,1:T(8,128)S(1)}, f32[256,384]{0,1:T(8,128)S(1)}, u32[]{:S(2)}, u32[]{:S(2)}) collective-permute-start(f32[256,384]{0,1:T(8,128)S(1)} %get-tuple-element.60), channel_id=1, source_target_pairs={{0,1},{1,2},{2,3},{3,4},{4,5},{5,6},{6,7},{8,9},{9,10},{10,11},{11... | collective-permute-start | bytes 1179656 | tf_op jit(solution)/shard_map/ppermute | solution.py:14
  317.0 8.7 %copy-start.11 = (f32[512,384]{0,1:T(8,128)}, f32[512,384]{0,1:T(8,128)S(1)}, u32[]{:S(2)}) copy-start(f32[512,384]{0,1:T(8,128)S(1)} %slice.132) | copy-start | bytes 2359300
  325.3 25.8 %copy-start.28 = (f32[256,384]{0,1:T(8,128)}, f32[256,384]{0,1:T(8,128)S(1)}, u32[]{:S(2)}) copy-start(f32[256,384]{0,1:T(8,128)S(1)} %get-tuple-element.29) | copy-start | bytes 1179652
  352.1 163.9 %all-reduce.12.cloned.1.call-start = ((), (), s32[]{:S(2)}) async-start(), calls=%async_computation.7 | async-start | bytes 196608 | tf_op jit(solution)/shard_map/psum | solution.py:107
  403.9 1.2 copy-start.29
  407.9 11.9 %collective-permute-start.13 = (f32[256,384]{0,1:T(8,128)S(1)}, f32[256,384]{0,1:T(8,128)S(1)}, u32[]{:S(2)}, u32[]{:S(2)}) collective-permute-start(f32[256,384]{0,1:T(8,128)S(1)} %get-tuple-element.27), channel_id=1, source_target_pairs={{1,0},{2,1},{3,2},{4,3},{5,4},{6,5},{7,6},{9,8},{10,9},{11,10},{12... | collective-permute-start | bytes 1179656 | tf_op jit(solution)/shard_map/ppermute | solution.py:14
  420.0 11.9 %collective-permute-start.12 = (f32[256,384]{0,1:T(8,128)S(1)}, f32[256,384]{0,1:T(8,128)S(1)}, u32[]{:S(2)}, u32[]{:S(2)}) collective-permute-start(f32[256,384]{0,1:T(8,128)S(1)} %get-tuple-element.58), channel_id=1, source_target_pairs={{0,1},{1,2},{2,3},{3,4},{4,5},{5,6},{6,7},{8,9},{9,10},{10,11},{11... | collective-permute-start | bytes 1179656 | tf_op jit(solution)/shard_map/ppermute | solution.py:14
  423.0 9.2 %copy-start.31 = (f32[256,384]{0,1:T(8,128)S(1)}, f32[256,384]{0,1:T(8,128)}, u32[]{:S(2)}) copy-start(f32[256,384]{0,1:T(8,128)} %copy-done.30) | copy-start | bytes 1179652
  423.0 9.2 %copy-start.34 = (f32[256,384]{0,1:T(8,128)S(1)}, f32[256,384]{0,1:T(8,128)}, u32[]{:S(2)}) copy-start(f32[256,384]{0,1:T(8,128)} %copy-done.33) | copy-start | bytes 1179652
  423.0 9.2 %copy-start.42 = (f32[512,384]{0,1:T(8,128)S(1)}, f32[512,384]{0,1:T(8,128)}, u32[]{:S(2)}) copy-start(f32[512,384]{0,1:T(8,128)} %copy-done.41) | copy-start | bytes 2359300
  424.0 9.4 %copy-start.44 = (f32[512,384]{0,1:T(8,128)}, f32[512,384]{0,1:T(8,128)S(1)}, u32[]{:S(2)}) copy-start(f32[512,384]{0,1:T(8,128)S(1)} %get-tuple-element.22) | copy-start | bytes 2359300
  424.0 8.2 %copy-start.3 = (f32[1,1,1024,384]{2,3,1,0:T(8,128)S(1)}, f32[1,1,1024,384]{2,3,1,0:T(8,128)}, u32[]{:S(2)}) copy-start(f32[1,1,1024,384]{2,3,1,0:T(8,128)} %copy.14) | copy-start | bytes 4718596
  424.0 8.2 %copy-start.15 = (f32[512,384]{0,1:T(8,128)S(1)}, f32[512,384]{0,1:T(8,128)}, u32[]{:S(2)}) copy-start(f32[512,384]{0,1:T(8,128)} %copy-done.13) | copy-start | bytes 2359300
  433.4 10.1 %collective-permute-start.15 = (f32[256,384]{0,1:T(8,128)S(1)}, f32[256,384]{0,1:T(8,128)S(1)}, u32[]{:S(2)}, u32[]{:S(2)}) collective-permute-start(f32[256,384]{0,1:T(8,128)S(1)} %get-tuple-element.21), channel_id=1, source_target_pairs={{1,0},{2,1},{3,2},{4,3},{5,4},{6,5},{7,6},{9,8},{10,9},{11,10},{12... | collective-permute-start | bytes 1179656 | tf_op jit(solution)/shard_map/ppermute | solution.py:14
  443.9 10.7 %collective-permute-start.14 = (f32[256,384]{0,1:T(8,128)S(1)}, f32[256,384]{0,1:T(8,128)S(1)}, u32[]{:S(2)}, u32[]{:S(2)}) collective-permute-start(f32[256,384]{0,1:T(8,128)S(1)} %get-tuple-element.56), channel_id=1, source_target_pairs={{0,1},{1,2},{2,3},{3,4},{4,5},{5,6},{6,7},{8,9},{9,10},{10,11},{11... | collective-permute-start | bytes 1179656 | tf_op jit(solution)/shard_map/ppermute | solution.py:14
  446.4 8.7 %copy-start.7 = (f32[512,384]{0,1:T(8,128)}, f32[512,384]{0,1:T(8,128)S(1)}, u32[]{:S(2)}) copy-start(f32[512,384]{0,1:T(8,128)S(1)} %slice.138) | copy-start | bytes 2359300
  454.8 25.8 %copy-start.24 = (f32[256,384]{0,1:T(8,128)}, f32[256,384]{0,1:T(8,128)S(1)}, u32[]{:S(2)}) copy-start(f32[256,384]{0,1:T(8,128)S(1)} %get-tuple-element.19) | copy-start | bytes 1179652
  533.4 1.2 copy-start.25
  537.3 11.8 %collective-permute-start.17 = (f32[256,384]{0,1:T(8,128)S(1)}, f32[256,384]{0,1:T(8,128)S(1)}, u32[]{:S(2)}, u32[]{:S(2)}) collective-permute-start(f32[256,384]{0,1:T(8,128)S(1)} %get-tuple-element.17), channel_id=1, source_target_pairs={{1,0},{2,1},{3,2},{4,3},{5,4},{6,5},{7,6},{9,8},{10,9},{11,10},{12... | collective-permute-start | bytes 1179656 | tf_op jit(solution)/shard_map/ppermute | solution.py:14
  549.2 12.5 %copy-start.45 = (f32[512,384]{0,1:T(8,128)S(1)}, f32[512,384]{0,1:T(8,128)}, u32[]{:S(2)}) copy-start(f32[512,384]{0,1:T(8,128)} %copy-done.44) | copy-start | bytes 2359300
  549.5 11.9 %collective-permute-start.16 = (f32[256,384]{0,1:T(8,128)S(1)}, f32[256,384]{0,1:T(8,128)S(1)}, u32[]{:S(2)}, u32[]{:S(2)}) collective-permute-start(f32[256,384]{0,1:T(8,128)S(1)} %get-tuple-element.54), channel_id=1, source_target_pairs={{0,1},{1,2},{2,3},{3,4},{4,5},{5,6},{6,7},{8,9},{9,10},{10,11},{11... | collective-permute-start | bytes 1179656 | tf_op jit(solution)/shard_map/ppermute | solution.py:14
  552.5 9.2 %copy-start.32 = (f32[256,384]{0,1:T(8,128)S(1)}, f32[256,384]{0,1:T(8,128)}, u32[]{:S(2)}) copy-start(f32[256,384]{0,1:T(8,128)} %copy-done.30) | copy-start | bytes 1179652
  552.5 9.2 %copy-start.35 = (f32[256,384]{0,1:T(8,128)S(1)}, f32[256,384]{0,1:T(8,128)}, u32[]{:S(2)}) copy-start(f32[256,384]{0,1:T(8,128)} %copy-done.33) | copy-start | bytes 1179652
  552.5 9.2 %copy-start.37 = (f32[256,384]{0,1:T(8,128)S(1)}, f32[256,384]{0,1:T(8,128)}, u32[]{:S(2)}) copy-start(f32[256,384]{0,1:T(8,128)} %copy-done.36) | copy-start | bytes 1179652
  552.5 9.2 %copy-start.39 = (f32[256,384]{0,1:T(8,128)S(1)}, f32[256,384]{0,1:T(8,128)}, u32[]{:S(2)}) copy-start(f32[256,384]{0,1:T(8,128)} %copy-done.38) | copy-start | bytes 1179652
  552.5 9.2 %copy-start.43 = (f32[512,384]{0,1:T(8,128)S(1)}, f32[512,384]{0,1:T(8,128)}, u32[]{:S(2)}) copy-start(f32[512,384]{0,1:T(8,128)} %copy-done.41) | copy-start | bytes 2359300
  552.6 9.1 %copy-start.4 = (f32[1,1,1024,384]{2,3,1,0:T(8,128)S(1)}, f32[1,1,1024,384]{2,3,1,0:T(8,128)}, u32[]{:S(2)}) copy-start(f32[1,1,1024,384]{2,3,1,0:T(8,128)} %copy.14) | copy-start | bytes 4718596
  552.6 9.1 %copy-start.16 = (f32[512,384]{0,1:T(8,128)S(1)}, f32[512,384]{0,1:T(8,128)}, u32[]{:S(2)}) copy-start(f32[512,384]{0,1:T(8,128)} %copy-done.13) | copy-start | bytes 2359300
  563.0 13.8 %copy-start.6 = (f32[1024,384]{0,1:T(8,128)}, f32[1024,384]{0,1:T(8,128)S(1)}, u32[]{:S(2)}) copy-start(f32[1024,384]{0,1:T(8,128)S(1)} %bitcast_subtract_fusion) | copy-start | bytes 4718596
  563.1 10.1 %collective-permute-start.19 = (f32[256,384]{0,1:T(8,128)S(1)}, f32[256,384]{0,1:T(8,128)S(1)}, u32[]{:S(2)}, u32[]{:S(2)}) collective-permute-start(f32[256,384]{0,1:T(8,128)S(1)} %get-tuple-element.11), channel_id=1, source_target_pairs={{1,0},{2,1},{3,2},{4,3},{5,4},{6,5},{7,6},{9,8},{10,9},{11,10},{12... | collective-permute-start | bytes 1179656 | tf_op jit(solution)/shard_map/ppermute | solution.py:14
  573.2 3.6 copy-start.17
  573.2 3.6 copy-start.18
  573.2 3.6 copy-start.19
  574.3 10.9 %collective-permute-start.18 = (f32[256,384]{0,1:T(8,128)}, f32[256,384]{0,1:T(8,128)}, u32[]{:S(2)}, u32[]{:S(2)}) collective-permute-start(f32[256,384]{0,1:T(8,128)} %get-tuple-element.52), channel_id=1, source_target_pairs={{0,1},{1,2},{2,3},{3,4},{4,5},{5,6},{6,7},{8,9},{9,10},{10,11},{11... | collective-permute-start | bytes 1179656 | tf_op jit(solution)/shard_map/ppermute | solution.py:14
  581.5 5.1 slice-start
  (12 other events, 12.7 us)
Sparse Core Ops, SparseCore 0:
  92.3 35.5 all-reduce.5
  222.9 34.2 all-reduce.7
  352.2 34.2 all-reduce.9
  481.7 34.2 all-reduce.11
where the time goes:
time: 599 us; the launch traced here: 598 us
  waiting for transfers between devices  271 us (45%)
  blocking collectives  179 us (30%)
  starting transfers between devices  55.8 us (9%)
  matrix products  30 us (5%)
  local copies, waits for them, and re-layouts  23.2 us (4%)
  between operations  19.8 us (3%)
  other arithmetic  18.8 us (3%)
    psum x4, waiting for transfers between devices, on_device(): owned = lax.psum(owned, 'group')  138 us
    ppermute x18, waiting for transfers between devices, from_behind(): return lax.ppermute(block, axis, route)  133 us
    all_gather x4, blocking collectives, on_device(): all_terms = lax.all_gather(coarse_terms, 'sub', axis=0, tiled=True)  104 us
    all_to_all x4, blocking collectives, on_device(): lax.all_to_all(partial_vals, 'sub', split_axis=0, concat_axis=0, tiled=True)  59.6 us
    ppermute x18, starting transfers between devices, from_behind(): return lax.ppermute(block, axis, route)  49.6 us
    unnamed x108, local copies, waits for them, and re-layouts  15.7 us
    unnamed x1, blocking collectives  14.9 us
  transfers between devices with their start and end apart: 24, of which 21 were waited for; matrix products, arithmetic and copies ran while one was open for 4% of the time, Pallas kernels for 0%

commit v1 on v0

--- a/solution.py
+++ b/solution.py
@@ -1,3 +1,4 @@
+import functools
 import jax
 import jax.numpy as jnp
 from jax import lax
@@ -6,6 +7,14 @@
 MAXSH = 256
 ITERS = 4
 OMEGA = 0.6
+
+
+def _settle_boxes(mine, across):
+    arr_next = lax.all_gather(mine, across)
+    return jnp.sum(arr_next, axis=0)
+
+
+joints_close = functools.partial(_settle_boxes, across="group")
 
 
 def from_behind(block, axis, distance):
@@ -104,7 +113,7 @@
             jnp.float32
         )
         owned = lax.dot_general(own_select, all_terms, (((0,), (0,)), ((), ())), precision=highest)
-        owned = lax.psum(owned, "group")
+        owned = joints_close(owned)
         columns = jnp.take(coarse_inverse, dof_index, axis=1)
         partial_vals = lax.dot_general(columns, owned, (((0,), (0,)), ((), ())), precision=highest)
         partial_vals = partial_vals.reshape(-1, coarse_terms.shape[0], cases)

time: 599 us -> 503 us (0.84)
  waiting for transfers between devices: 271 us -> 142 us
  blocking collectives: 179 us -> 224 us
  between operations: 19.8 us -> 6.26 us
    psum x4 -> x0, waiting for transfers between devices: 138 us -> none  [on_device(): owned = lax.psum(owned, 'group')]
    all_gather x0 -> x4, blocking collectives: none -> 26.4 us  [_settle_boxes(): arr_next = lax.all_gather(mine, across)]
    all_to_all x4, blocking collectives: 59.6 us -> 75.5 us  [on_device(): lax.all_to_all(partial_vals, 'sub', split_axis=0, concat_axis=0, tiled=True)]
    ppermute x18, waiting for transfers between devices: 133 us -> 142 us  [from_behind(): return lax.ppermute(block, axis, route)]
    reduce_sum x0 -> x4, other arithmetic: none -> 6.64 us  [_settle_boxes(): return jnp.sum(arr_next, axis=0)]
    unnamed x108 -> x102, local copies, waits for them, and re-layouts: 15.7 us -> 14.2 us
  transfers between devices with their start and end apart: 24 -> 20, of which waited for: 21 -> 17; matrix products, arithmetic and copies ran while one was open for 4% -> 4% of each run, Pallas kernels for 0% -> 0%
where the time goes in v1:
time: 503 us; the launch traced here: 501 us
  blocking collectives  224 us (45%)
  waiting for transfers between devices  142 us (28%)
  starting transfers between devices  57.5 us (11%)
  matrix products  27.1 us (5%)
  other arithmetic  24.6 us (5%)
  local copies, waits for them, and re-layouts  20.7 us (4%)
  between operations  6.26 us (1%)
    ppermute x18, waiting for transfers between devices, from_behind(): return lax.ppermute(block, axis, route)  142 us
    all_gather x4, blocking collectives, on_device(): all_terms = lax.all_gather(coarse_terms, 'sub', axis=0, tiled=True)  105 us
    all_to_all x4, blocking collectives, on_device(): lax.all_to_all(partial_vals, 'sub', split_axis=0, concat_axis=0, tiled=True)  75.5 us
    ppermute x18, starting transfers between devices, from_behind(): return lax.ppermute(block, axis, route)  51.5 us
    all_gather x4, blocking collectives, _settle_boxes(): arr_next = lax.all_gather(mine, across)  26.4 us
    unnamed x1, blocking collectives  16.7 us
    unnamed x102, local copies, waits for them, and re-layouts  14.2 us
    dot_general x4, matrix products, on_device(): correction = jnp.dot(neumann, weighted, preferred_element_type=jnp.float32)  10.6 us
  transfers between devices with their start and end apart: 20, of which 17 were waited for; matrix products, arithmetic and copies ran while one was open for 4% of the time, Pallas kernels for 0%

profile of v1, /device:TPU:16, one launch (start us, length us, event | category | flops | bytes accessed | tf_op | source)
XLA Modules:
  0.0 501.4 jit_solution(1694790833766985697)
XLA Ops:
  0.6 3.4 collective-permute-start.1
  4.1 2.6 collective-permute-start
  6.6 3.0 copy.18
  9.7 2.4 bitcast_subtract_fusion.4
  13.3 4.2 collective-permute-start.3
  20.0 16.7 %all-reduce = f32[256]{0:T(256)S(1)} all-reduce(f32[256]{0:T(256)S(1)} %bitcast_dynamic-update-slice_fusion), channel_id=2, replica_groups=mesh['group'=4,'sub'=8] {'sub'}, use_global_device_ids=true, to_apply=%add | all-reduce | flops 256 | bytes 2048
  38.6 1.9 collective-permute-start.2
  46.6 2.9 collective-permute-done.2
  49.5 1.7 slice_add_fusion.8
  51.5 27.6 %all_gather.43 = f32[256,384]{1,0:T(8,128)S(1)} all-gather(f32[32,384]{1,0:T(8,128)S(1)} %convolution_bitcast_fusion.3), channel_id=1, replica_groups=mesh['group'=4,'sub'=8] {'sub'}, dimensions={0}, use_global_device_ids=true | all-gather | bytes 442368 | tf_op jit(solution)/shard_map/all_gather | solution.py:108
  79.5 6.6 %all-gather.1 = f32[256,384]{1,0:T(8,128)} all-gather(f32[64,384]{1,0:T(8,128)S(1)} %fusion.97), channel_id=3, replica_groups=mesh['group'=4,'sub'=8] {'group'}, dimensions={0}, use_global_device_ids=true | all-gather | bytes 491520 | tf_op jit(solution)/shard_map/all_gather | solution.py:13
  86.1 1.7 reduce_sum.72
  89.1 18.8 %all_to_all.20 = f32[8,32,384]{2,1,0:T(8,128)} all-to-all(f32[8,32,384]{2,1,0:T(8,128)S(1)} %fusion.107), channel_id=1, replica_groups=mesh['group'=4,'sub'=8] {'sub'}, dimensions={0} | all-to-all | bytes 786432 | tf_op jit(solution)/shard_map/all_to_all | solution.py:120
  110.0 2.6 multiply_bitcast_fusion.3
  112.7 3.3 collective-permute-start.5
  116.0 9.6 %collective-permute-done.5 = f32[256,384]{0,1:T(8,128)S(1)} collective-permute-done((f32[256,384]{0,1:T(8,128)S(1)}, f32[256,384]{0,1:T(8,128)S(1)}, u32[]{:S(2)}, u32[]{:S(2)}) %collective-permute-start.5) | collective-permute-done | bytes 393248 | tf_op jit(solution)/shard_map/ppermute | solution.py:23
  125.9 3.0 collective-permute-start.4
  129.9 8.9 %collective-permute-done.4 = f32[256,384]{0,1:T(8,128)S(1)} collective-permute-done((f32[256,384]{0,1:T(8,128)S(1)}, f32[256,384]{0,1:T(8,128)S(1)}, u32[]{:S(2)}, u32[]{:S(2)}) %collective-permute-start.4) | collective-permute-done | bytes 393248 | tf_op jit(solution)/shard_map/ppermute | solution.py:23
  140.3 1.9 collective-permute-start.7
  142.2 9.3 %collective-permute-done.7 = f32[256,384]{0,1:T(8,128)S(1)} collective-permute-done((f32[256,384]{0,1:T(8,128)S(1)}, f32[256,384]{0,1:T(8,128)S(1)}, u32[]{:S(2)}, u32[]{:S(2)}) %collective-permute-start.7) | collective-permute-done | bytes 393248 | tf_op jit(solution)/shard_map/ppermute | solution.py:23
  151.8 3.0 collective-permute-start.6
  154.9 8.2 %collective-permute-done.6 = f32[256,384]{0,1:T(8,128)S(1)} collective-permute-done((f32[256,384]{0,1:T(8,128)S(1)}, f32[256,384]{0,1:T(8,128)S(1)}, u32[]{:S(2)}, u32[]{:S(2)}) %collective-permute-start.6) | collective-permute-done | bytes 393248 | tf_op jit(solution)/shard_map/ppermute | solution.py:23
  163.7 25.8 %all_gather.46 = f32[256,384]{1,0:T(8,128)S(1)} all-gather(f32[32,384]{1,0:T(8,128)S(1)} %convolution_bitcast_fusion.2), channel_id=1, replica_groups=mesh['group'=4,'sub'=8] {'sub'}, dimensions={0}, use_global_device_ids=true | all-gather | bytes 442368 | tf_op jit(solution)/shard_map/all_gather | solution.py:108
  189.8 6.6 %all-gather.2 = f32[256,384]{1,0:T(8,128)} all-gather(f32[64,384]{1,0:T(8,128)S(1)} %fusion.95), channel_id=4, replica_groups=mesh['group'=4,'sub'=8] {'group'}, dimensions={0}, use_global_device_ids=true | all-gather | bytes 491520 | tf_op jit(solution)/shard_map/all_gather | solution.py:13
  196.4 1.7 reduce_sum.74
  199.4 18.9 %all_to_all.21 = f32[8,32,384]{2,1,0:T(8,128)} all-to-all(f32[8,32,384]{2,1,0:T(8,128)S(1)} %fusion.105), channel_id=1, replica_groups=mesh['group'=4,'sub'=8] {'sub'}, dimensions={0} | all-to-all | bytes 786432 | tf_op jit(solution)/shard_map/all_to_all | solution.py:120
  220.6 2.7 multiply_bitcast_fusion.2
  223.3 3.3 collective-permute-start.9
  226.6 9.5 %collective-permute-done.9 = f32[256,384]{0,1:T(8,128)S(1)} collective-permute-done((f32[256,384]{0,1:T(8,128)S(1)}, f32[256,384]{0,1:T(8,128)S(1)}, u32[]{:S(2)}, u32[]{:S(2)}) %collective-permute-start.9) | collective-permute-done | bytes 393248 | tf_op jit(solution)/shard_map/ppermute | solution.py:23
  236.4 3.2 collective-permute-start.8
  240.7 8.5 %collective-permute-done.8 = f32[256,384]{0,1:T(8,128)S(1)} collective-permute-done((f32[256,384]{0,1:T(8,128)S(1)}, f32[256,384]{0,1:T(8,128)S(1)}, u32[]{:S(2)}, u32[]{:S(2)}) %collective-permute-start.8) | collective-permute-done | bytes 393248 | tf_op jit(solution)/shard_map/ppermute | solution.py:23
  250.7 1.9 collective-permute-start.11
  252.6 9.2 %collective-permute-done.11 = f32[256,384]{0,1:T(8,128)S(1)} collective-permute-done((f32[256,384]{0,1:T(8,128)S(1)}, f32[256,384]{0,1:T(8,128)S(1)}, u32[]{:S(2)}, u32[]{:S(2)}) %collective-permute-start.11) | collective-permute-done | bytes 393248 | tf_op jit(solution)/shard_map/ppermute | solution.py:23
  262.1 3.0 collective-permute-start.10
  265.1 8.0 %collective-permute-done.10 = f32[256,384]{0,1:T(8,128)S(1)} collective-permute-done((f32[256,384]{0,1:T(8,128)S(1)}, f32[256,384]{0,1:T(8,128)S(1)}, u32[]{:S(2)}, u32[]{:S(2)}) %collective-permute-start.10) | collective-permute-done | bytes 393248 | tf_op jit(solution)/shard_map/ppermute | solution.py:23
  273.8 26.0 %all_gather.49 = f32[256,384]{1,0:T(8,128)S(1)} all-gather(f32[32,384]{1,0:T(8,128)S(1)} %convolution_bitcast_fusion.1), channel_id=1, replica_groups=mesh['group'=4,'sub'=8] {'sub'}, dimensions={0}, use_global_device_ids=true | all-gather | bytes 442368 | tf_op jit(solution)/shard_map/all_gather | solution.py:108
  300.2 6.6 %all-gather.3 = f32[256,384]{1,0:T(8,128)} all-gather(f32[64,384]{1,0:T(8,128)S(1)} %fusion.93), channel_id=5, replica_groups=mesh['group'=4,'sub'=8] {'group'}, dimensions={0}, use_global_device_ids=true | all-gather | bytes 491520 | tf_op jit(solution)/shard_map/all_gather | solution.py:13
  306.8 1.7 reduce_sum.76
  309.8 18.8 %all_to_all.22 = f32[8,32,384]{2,1,0:T(8,128)} all-to-all(f32[8,32,384]{2,1,0:T(8,128)S(1)} %fusion.103), channel_id=1, replica_groups=mesh['group'=4,'sub'=8] {'sub'}, dimensions={0} | all-to-all | bytes 786432 | tf_op jit(solution)/shard_map/all_to_all | solution.py:120
  330.9 2.7 multiply_bitcast_fusion.1
  333.6 3.3 collective-permute-start.13
  336.9 9.6 %collective-permute-done.13 = f32[256,384]{0,1:T(8,128)S(1)} collective-permute-done((f32[256,384]{0,1:T(8,128)S(1)}, f32[256,384]{0,1:T(8,128)S(1)}, u32[]{:S(2)}, u32[]{:S(2)}) %collective-permute-start.13) | collective-permute-done | bytes 393248 | tf_op jit(solution)/shard_map/ppermute | solution.py:23
  346.8 3.0 collective-permute-start.12
  350.9 8.9 %collective-permute-done.12 = f32[256,384]{0,1:T(8,128)S(1)} collective-permute-done((f32[256,384]{0,1:T(8,128)S(1)}, f32[256,384]{0,1:T(8,128)S(1)}, u32[]{:S(2)}, u32[]{:S(2)}) %collective-permute-start.12) | collective-permute-done | bytes 393248 | tf_op jit(solution)/shard_map/ppermute | solution.py:23
  361.3 1.9 collective-permute-start.15
  363.2 9.3 %collective-permute-done.15 = f32[256,384]{0,1:T(8,128)S(1)} collective-permute-done((f32[256,384]{0,1:T(8,128)S(1)}, f32[256,384]{0,1:T(8,128)S(1)}, u32[]{:S(2)}, u32[]{:S(2)}) %collective-permute-start.15) | collective-permute-done | bytes 393248 | tf_op jit(solution)/shard_map/ppermute | solution.py:23
  372.8 3.0 collective-permute-start.14
  375.9 8.1 %collective-permute-done.14 = f32[256,384]{0,1:T(8,128)S(1)} collective-permute-done((f32[256,384]{0,1:T(8,128)S(1)}, f32[256,384]{0,1:T(8,128)S(1)}, u32[]{:S(2)}, u32[]{:S(2)}) %collective-permute-start.14) | collective-permute-done | bytes 393248 | tf_op jit(solution)/shard_map/ppermute | solution.py:23
  384.7 25.8 %all_gather.52 = f32[256,384]{1,0:T(8,128)S(1)} all-gather(f32[32,384]{1,0:T(8,128)S(1)} %convolution_bitcast_fusion), channel_id=1, replica_groups=mesh['group'=4,'sub'=8] {'sub'}, dimensions={0}, use_global_device_ids=true | all-gather | bytes 442368 | tf_op jit(solution)/shard_map/all_gather | solution.py:108
  410.8 6.6 %all-gather.4 = f32[256,384]{1,0:T(8,128)} all-gather(f32[64,384]{1,0:T(8,128)S(1)} %fusion.91), channel_id=6, replica_groups=mesh['group'=4,'sub'=8] {'group'}, dimensions={0}, use_global_device_ids=true | all-gather | bytes 491520 | tf_op jit(solution)/shard_map/all_gather | solution.py:13
  417.4 1.7 reduce_sum.78
  420.4 18.9 %all_to_all.23 = f32[8,32,384]{2,1,0:T(8,128)} all-to-all(f32[8,32,384]{2,1,0:T(8,128)S(1)} %fusion.101), channel_id=1, replica_groups=mesh['group'=4,'sub'=8] {'sub'}, dimensions={0} | all-to-all | bytes 786432 | tf_op jit(solution)/shard_map/all_to_all | solution.py:120
  441.6 2.6 multiply_bitcast_fusion
  444.3 3.3 collective-permute-start.17
  447.6 9.5 %collective-permute-done.17 = f32[256,384]{0,1:T(8,128)S(1)} collective-permute-done((f32[256,384]{0,1:T(8,128)S(1)}, f32[256,384]{0,1:T(8,128)S(1)}, u32[]{:S(2)}, u32[]{:S(2)}) %collective-permute-start.17) | collective-permute-done | bytes 393248 | tf_op jit(solution)/shard_map/ppermute | solution.py:23
  457.4 3.2 collective-permute-start.16
  460.8 9.4 %collective-permute-done.16 = f32[256,384]{0,1:T(8,128)S(1)} collective-permute-done((f32[256,384]{0,1:T(8,128)S(1)}, f32[256,384]{0,1:T(8,128)S(1)}, u32[]{:S(2)}, u32[]{:S(2)}) %collective-permute-start.16) | collective-permute-done | bytes 393248 | tf_op jit(solution)/shard_map/ppermute | solution.py:23
  471.9 1.9 collective-permute-start.19
  473.9 9.2 %collective-permute-done.19 = f32[256,384]{0,1:T(8,128)S(1)} collective-permute-done((f32[256,384]{0,1:T(8,128)S(1)}, f32[256,384]{0,1:T(8,128)S(1)}, u32[]{:S(2)}, u32[]{:S(2)}) %collective-permute-start.19) | collective-permute-done | bytes 393248 | tf_op jit(solution)/shard_map/ppermute | solution.py:23
  484.1 3.0 collective-permute-start.18
  487.1 1.7 fusion.21
  488.8 3.0 copy.20
  491.8 3.7 collective-permute-done.18
  498.4 3.0 copy.21
  (174 shorter events, 40.4 us)
Async XLA Ops:
  0.6 9.0 %copy-start = (bf16[1,1,1024,1024]{3,2,1,0:T(8,128)(2,1)S(1)}, bf16[1,1,1024,1024]{3,2,1,0:T(8,128)(2,1)}, u32[]{:S(2)}) copy-start(bf16[1,1,1024,1024]{3,2,1,0:T(8,128)(2,1)} %param.15) | copy-start | bytes 6291460
  0.6 44.0 %collective-permute-start.1 = (f32[1,1]{1,0:T(1,128)}, f32[1,1]{1,0:T(1,128)}, u32[]{:S(2)}, u32[]{:S(2)}) collective-permute-start(f32[1,1]{1,0:T(1,128)} %param.13), channel_id=1, source_target_pairs={{1,0},{2,1},{3,2},{4,3},{5,4},{6,5},{7,6},{9,8},{10,9},{11,10},{12... | collective-permute-start | bytes 20 | tf_op jit(solution)/shard_map/ppermute | solution.py:34
  4.1 41.2 %collective-permute-start = (f32[1,1]{1,0:T(1,128)}, f32[1,1]{1,0:T(1,128)}, u32[]{:S(2)}, u32[]{:S(2)}) collective-permute-start(f32[1,1]{1,0:T(1,128)} %param.13), channel_id=1, source_target_pairs={{0,1},{1,2},{2,3},{3,4},{4,5},{5,6},{6,7},{8,9},{9,10},{10,11},{11... | collective-permute-start | bytes 20 | tf_op jit(solution)/shard_map/ppermute | solution.py:33
  12.1 1.1 copy-start.5
  13.2 4.3 copy-start.45
  13.2 5.5 %copy-start.47 = (u32[32]{0:T(128)S(1)}, u32[32]{0:T(128)}, u32[]{:S(2)}) copy-start(u32[32]{0:T(128)} %constant.58) | copy-start | bytes 388
  13.2 6.7 %copy-start.46 = (s32[1,1,32]{2,1,0:T(1,128)S(1)}, s32[1,1,32]{2,1,0:T(1,128)}, u32[]{:S(2)}) copy-start(s32[1,1,32]{2,1,0:T(1,128)} %param.18) | copy-start | bytes 388
  13.3 24.1 %collective-permute-start.3 = (f32[256,384]{0,1:T(8,128)S(1)}, f32[256,384]{0,1:T(8,128)S(1)}, u32[]{:S(2)}, u32[]{:S(2)}) collective-permute-start(f32[256,384]{0,1:T(8,128)S(1)} %get-tuple-element.53), channel_id=1, source_target_pairs={{1,0},{2,1},{3,2},{4,3},{5,4},{6,5},{7,6},{9,8},{10,9},{11,10},{12... | collective-permute-start | bytes 1179656 | tf_op jit(solution)/shard_map/ppermute | solution.py:23
  37.4 5.6 %copy-start.44 = (f32[64,512]{1,0:T(8,128)S(1)}, f32[64,512]{1,0:T(8,128)}, u32[]{:S(2)}) copy-start(f32[64,512]{1,0:T(8,128)} %param.19) | copy-start | bytes 393220
  38.6 10.9 %collective-permute-start.2 = (f32[256,384]{0,1:T(8,128)}, f32[256,384]{0,1:T(8,128)}, u32[]{:S(2)}, u32[]{:S(2)}) collective-permute-start(f32[256,384]{0,1:T(8,128)} %get-tuple-element.72), channel_id=1, source_target_pairs={{0,1},{1,2},{2,3},{3,4},{4,5},{5,6},{6,7},{8,9},{9,10},{10,11},{11... | collective-permute-start | bytes 1179656 | tf_op jit(solution)/shard_map/ppermute | solution.py:23
  43.8 7.4 %copy-start.38 = (bf16[1,1,32,1024]{3,2,1,0:T(8,128)(2,1)S(1)}, bf16[1,1,32,1024]{3,2,1,0:T(8,128)(2,1)}, u32[]{:S(2)}) copy-start(bf16[1,1,32,1024]{3,2,1,0:T(8,128)(2,1)} %param.17) | copy-start | bytes 196612
  51.2 28.4 %copy-start.22 = (f32[256,384]{0,1:T(8,128)}, f32[256,384]{0,1:T(8,128)S(1)}, u32[]{:S(2)}) copy-start(f32[256,384]{0,1:T(8,128)S(1)} %get-tuple-element.51) | copy-start | bytes 1179652
  112.7 12.9 %collective-permute-start.5 = (f32[256,384]{0,1:T(8,128)S(1)}, f32[256,384]{0,1:T(8,128)S(1)}, u32[]{:S(2)}, u32[]{:S(2)}) collective-permute-start(f32[256,384]{0,1:T(8,128)S(1)} %get-tuple-element.49), channel_id=1, source_target_pairs={{1,0},{2,1},{3,2},{4,3},{5,4},{6,5},{7,6},{9,8},{10,9},{11,10},{12... | collective-permute-start | bytes 1179656 | tf_op jit(solution)/shard_map/ppermute | solution.py:23
  125.9 13.0 %collective-permute-start.4 = (f32[256,384]{0,1:T(8,128)S(1)}, f32[256,384]{0,1:T(8,128)S(1)}, u32[]{:S(2)}, u32[]{:S(2)}) collective-permute-start(f32[256,384]{0,1:T(8,128)S(1)} %get-tuple-element.68), channel_id=1, source_target_pairs={{0,1},{1,2},{2,3},{3,4},{4,5},{5,6},{6,7},{8,9},{9,10},{10,11},{11... | collective-permute-start | bytes 1179656 | tf_op jit(solution)/shard_map/ppermute | solution.py:23
  129.9 10.3 %copy-start.13 = (f32[512,384]{0,1:T(8,128)}, f32[512,384]{0,1:T(8,128)S(1)}, u32[]{:S(2)}) copy-start(f32[512,384]{0,1:T(8,128)S(1)} %get-tuple-element.44) | copy-start | bytes 2359300
  129.9 9.2 %copy-start.1 = (f32[1,1,1024,384]{2,3,1,0:T(8,128)S(1)}, f32[1,1,1024,384]{2,3,1,0:T(8,128)}, u32[]{:S(2)}) copy-start(f32[1,1,1024,384]{2,3,1,0:T(8,128)} %copy.18) | copy-start | bytes 4718596
  140.3 11.2 %collective-permute-start.7 = (f32[256,384]{0,1:T(8,128)S(1)}, f32[256,384]{0,1:T(8,128)S(1)}, u32[]{:S(2)}, u32[]{:S(2)}) collective-permute-start(f32[256,384]{0,1:T(8,128)S(1)} %get-tuple-element.43), channel_id=1, source_target_pairs={{1,0},{2,1},{3,2},{4,3},{5,4},{6,5},{7,6},{9,8},{10,9},{11,10},{12... | collective-permute-start | bytes 1179656 | tf_op jit(solution)/shard_map/ppermute | solution.py:23
  151.8 11.2 %collective-permute-start.6 = (f32[256,384]{0,1:T(8,128)S(1)}, f32[256,384]{0,1:T(8,128)S(1)}, u32[]{:S(2)}, u32[]{:S(2)}) collective-permute-start(f32[256,384]{0,1:T(8,128)S(1)} %get-tuple-element.66), channel_id=1, source_target_pairs={{0,1},{1,2},{2,3},{3,4},{4,5},{5,6},{6,7},{8,9},{9,10},{10,11},{11... | collective-permute-start | bytes 1179656 | tf_op jit(solution)/shard_map/ppermute | solution.py:23
  154.9 8.8 %copy-start.9 = (f32[512,384]{0,1:T(8,128)}, f32[512,384]{0,1:T(8,128)S(1)}, u32[]{:S(2)}) copy-start(f32[512,384]{0,1:T(8,128)S(1)} %slice.126) | copy-start | bytes 2359300
  163.3 26.5 %copy-start.24 = (f32[256,384]{0,1:T(8,128)}, f32[256,384]{0,1:T(8,128)S(1)}, u32[]{:S(2)}) copy-start(f32[256,384]{0,1:T(8,128)S(1)} %get-tuple-element.41) | copy-start | bytes 1179652
  219.4 1.2 copy-start.25
  223.3 12.8 %collective-permute-start.9 = (f32[256,384]{0,1:T(8,128)S(1)}, f32[256,384]{0,1:T(8,128)S(1)}, u32[]{:S(2)}, u32[]{:S(2)}) collective-permute-start(f32[256,384]{0,1:T(8,128)S(1)} %get-tuple-element.39), channel_id=1, source_target_pairs={{1,0},{2,1},{3,2},{4,3},{5,4},{6,5},{7,6},{9,8},{10,9},{11,10},{12... | collective-permute-start | bytes 1179656 | tf_op jit(solution)/shard_map/ppermute | solution.py:23
  236.4 12.8 %collective-permute-start.8 = (f32[256,384]{0,1:T(8,128)S(1)}, f32[256,384]{0,1:T(8,128)S(1)}, u32[]{:S(2)}, u32[]{:S(2)}) collective-permute-start(f32[256,384]{0,1:T(8,128)S(1)} %get-tuple-element.64), channel_id=1, source_target_pairs={{0,1},{1,2},{2,3},{3,4},{4,5},{5,6},{6,7},{8,9},{9,10},{10,11},{11... | collective-permute-start | bytes 1179656 | tf_op jit(solution)/shard_map/ppermute | solution.py:23
  240.7 9.9 %copy-start.39 = (f32[512,384]{0,1:T(8,128)}, f32[512,384]{0,1:T(8,128)S(1)}, u32[]{:S(2)}) copy-start(f32[512,384]{0,1:T(8,128)S(1)} %get-tuple-element.34) | copy-start | bytes 2359300
  240.7 8.8 %copy-start.2 = (f32[1,1,1024,384]{2,3,1,0:T(8,128)S(1)}, f32[1,1,1024,384]{2,3,1,0:T(8,128)}, u32[]{:S(2)}) copy-start(f32[1,1,1024,384]{2,3,1,0:T(8,128)} %copy.18) | copy-start | bytes 4718596
  240.7 8.8 %copy-start.14 = (f32[512,384]{0,1:T(8,128)S(1)}, f32[512,384]{0,1:T(8,128)}, u32[]{:S(2)}) copy-start(f32[512,384]{0,1:T(8,128)} %copy-done.13) | copy-start | bytes 2359300
  250.7 11.1 %collective-permute-start.11 = (f32[256,384]{0,1:T(8,128)S(1)}, f32[256,384]{0,1:T(8,128)S(1)}, u32[]{:S(2)}, u32[]{:S(2)}) collective-permute-start(f32[256,384]{0,1:T(8,128)S(1)} %get-tuple-element.33), channel_id=1, source_target_pairs={{1,0},{2,1},{3,2},{4,3},{5,4},{6,5},{7,6},{9,8},{10,9},{11,10},{12... | collective-permute-start | bytes 1179656 | tf_op jit(solution)/shard_map/ppermute | solution.py:23
  262.1 11.1 %collective-permute-start.10 = (f32[256,384]{0,1:T(8,128)S(1)}, f32[256,384]{0,1:T(8,128)S(1)}, u32[]{:S(2)}, u32[]{:S(2)}) collective-permute-start(f32[256,384]{0,1:T(8,128)S(1)} %get-tuple-element.62), channel_id=1, source_target_pairs={{0,1},{1,2},{2,3},{3,4},{4,5},{5,6},{6,7},{8,9},{9,10},{10,11},{11... | collective-permute-start | bytes 1179656 | tf_op jit(solution)/shard_map/ppermute | solution.py:23
  265.1 8.7 %copy-start.11 = (f32[512,384]{0,1:T(8,128)}, f32[512,384]{0,1:T(8,128)S(1)}, u32[]{:S(2)}) copy-start(f32[512,384]{0,1:T(8,128)S(1)} %slice.132) | copy-start | bytes 2359300
  273.5 26.7 %copy-start.26 = (f32[256,384]{0,1:T(8,128)}, f32[256,384]{0,1:T(8,128)S(1)}, u32[]{:S(2)}) copy-start(f32[256,384]{0,1:T(8,128)S(1)} %get-tuple-element.31) | copy-start | bytes 1179652
  329.7 1.2 copy-start.27
  333.6 12.9 %collective-permute-start.13 = (f32[256,384]{0,1:T(8,128)S(1)}, f32[256,384]{0,1:T(8,128)S(1)}, u32[]{:S(2)}, u32[]{:S(2)}) collective-permute-start(f32[256,384]{0,1:T(8,128)S(1)} %get-tuple-element.29), channel_id=1, source_target_pairs={{1,0},{2,1},{3,2},{4,3},{5,4},{6,5},{7,6},{9,8},{10,9},{11,10},{12... | collective-permute-start | bytes 1179656 | tf_op jit(solution)/shard_map/ppermute | solution.py:23
  346.8 12.9 %collective-permute-start.12 = (f32[256,384]{0,1:T(8,128)S(1)}, f32[256,384]{0,1:T(8,128)S(1)}, u32[]{:S(2)}, u32[]{:S(2)}) collective-permute-start(f32[256,384]{0,1:T(8,128)S(1)} %get-tuple-element.60), channel_id=1, source_target_pairs={{0,1},{1,2},{2,3},{3,4},{4,5},{5,6},{6,7},{8,9},{9,10},{10,11},{11... | collective-permute-start | bytes 1179656 | tf_op jit(solution)/shard_map/ppermute | solution.py:23
  349.8 10.2 %copy-start.29 = (f32[256,384]{0,1:T(8,128)S(1)}, f32[256,384]{0,1:T(8,128)}, u32[]{:S(2)}) copy-start(f32[256,384]{0,1:T(8,128)} %copy-done.28) | copy-start | bytes 1179652
  349.8 10.2 %copy-start.32 = (f32[256,384]{0,1:T(8,128)S(1)}, f32[256,384]{0,1:T(8,128)}, u32[]{:S(2)}) copy-start(f32[256,384]{0,1:T(8,128)} %copy-done.31) | copy-start | bytes 1179652
  349.8 10.2 %copy-start.40 = (f32[512,384]{0,1:T(8,128)S(1)}, f32[512,384]{0,1:T(8,128)}, u32[]{:S(2)}) copy-start(f32[512,384]{0,1:T(8,128)} %copy-done.39) | copy-start | bytes 2359300
  350.9 10.3 %copy-start.42 = (f32[512,384]{0,1:T(8,128)}, f32[512,384]{0,1:T(8,128)S(1)}, u32[]{:S(2)}) copy-start(f32[512,384]{0,1:T(8,128)S(1)} %get-tuple-element.24) | copy-start | bytes 2359300
  350.9 9.2 %copy-start.3 = (f32[1,1,1024,384]{2,3,1,0:T(8,128)S(1)}, f32[1,1,1024,384]{2,3,1,0:T(8,128)}, u32[]{:S(2)}) copy-start(f32[1,1,1024,384]{2,3,1,0:T(8,128)} %copy.18) | copy-start | bytes 4718596
  350.9 9.2 %copy-start.15 = (f32[512,384]{0,1:T(8,128)S(1)}, f32[512,384]{0,1:T(8,128)}, u32[]{:S(2)}) copy-start(f32[512,384]{0,1:T(8,128)} %copy-done.13) | copy-start | bytes 2359300
  360.0 1.2 copy-start.34
  360.0 1.2 copy-start.36
  361.3 11.2 %collective-permute-start.15 = (f32[256,384]{0,1:T(8,128)S(1)}, f32[256,384]{0,1:T(8,128)S(1)}, u32[]{:S(2)}, u32[]{:S(2)}) collective-permute-start(f32[256,384]{0,1:T(8,128)S(1)} %get-tuple-element.23), channel_id=1, source_target_pairs={{1,0},{2,1},{3,2},{4,3},{5,4},{6,5},{7,6},{9,8},{10,9},{11,10},{12... | collective-permute-start | bytes 1179656 | tf_op jit(solution)/shard_map/ppermute | solution.py:23
  372.8 11.2 %collective-permute-start.14 = (f32[256,384]{0,1:T(8,128)S(1)}, f32[256,384]{0,1:T(8,128)S(1)}, u32[]{:S(2)}, u32[]{:S(2)}) collective-permute-start(f32[256,384]{0,1:T(8,128)S(1)} %get-tuple-element.58), channel_id=1, source_target_pairs={{0,1},{1,2},{2,3},{3,4},{4,5},{5,6},{6,7},{8,9},{9,10},{10,11},{11... | collective-permute-start | bytes 1179656 | tf_op jit(solution)/shard_map/ppermute | solution.py:23
  375.9 8.8 %copy-start.7 = (f32[512,384]{0,1:T(8,128)}, f32[512,384]{0,1:T(8,128)S(1)}, u32[]{:S(2)}) copy-start(f32[512,384]{0,1:T(8,128)S(1)} %slice.138) | copy-start | bytes 2359300
  384.3 26.5 %copy-start.20 = (f32[256,384]{0,1:T(8,128)}, f32[256,384]{0,1:T(8,128)S(1)}, u32[]{:S(2)}) copy-start(f32[256,384]{0,1:T(8,128)S(1)} %get-tuple-element.21) | copy-start | bytes 1179652
  440.4 1.1 copy-start.8
  440.4 1.2 copy-start.21
  444.3 12.8 %collective-permute-start.17 = (f32[256,384]{0,1:T(8,128)S(1)}, f32[256,384]{0,1:T(8,128)S(1)}, u32[]{:S(2)}, u32[]{:S(2)}) collective-permute-start(f32[256,384]{0,1:T(8,128)S(1)} %get-tuple-element.19), channel_id=1, source_target_pairs={{1,0},{2,1},{3,2},{4,3},{5,4},{6,5},{7,6},{9,8},{10,9},{11,10},{12... | collective-permute-start | bytes 1179656 | tf_op jit(solution)/shard_map/ppermute | solution.py:23
  457.1 13.4 %copy-start.43 = (f32[512,384]{0,1:T(8,128)S(1)}, f32[512,384]{0,1:T(8,128)}, u32[]{:S(2)}) copy-start(f32[512,384]{0,1:T(8,128)} %copy-done.42) | copy-start | bytes 2359300
  457.4 12.8 %collective-permute-start.16 = (f32[256,384]{0,1:T(8,128)S(1)}, f32[256,384]{0,1:T(8,128)S(1)}, u32[]{:S(2)}, u32[]{:S(2)}) collective-permute-start(f32[256,384]{0,1:T(8,128)S(1)} %get-tuple-element.56), channel_id=1, source_target_pairs={{0,1},{1,2},{2,3},{3,4},{4,5},{5,6},{6,7},{8,9},{9,10},{10,11},{11... | collective-permute-start | bytes 1179656 | tf_op jit(solution)/shard_map/ppermute | solution.py:23
  460.6 9.9 %copy-start.30 = (f32[256,384]{0,1:T(8,128)S(1)}, f32[256,384]{0,1:T(8,128)}, u32[]{:S(2)}) copy-start(f32[256,384]{0,1:T(8,128)} %copy-done.28) | copy-start | bytes 1179652
  460.7 9.9 %copy-start.33 = (f32[256,384]{0,1:T(8,128)S(1)}, f32[256,384]{0,1:T(8,128)}, u32[]{:S(2)}) copy-start(f32[256,384]{0,1:T(8,128)} %copy-done.31) | copy-start | bytes 1179652
  460.7 9.9 %copy-start.35 = (f32[256,384]{0,1:T(8,128)S(1)}, f32[256,384]{0,1:T(8,128)}, u32[]{:S(2)}) copy-start(f32[256,384]{0,1:T(8,128)} %copy-done.34) | copy-start | bytes 1179652
  460.7 9.9 %copy-start.37 = (f32[256,384]{0,1:T(8,128)S(1)}, f32[256,384]{0,1:T(8,128)}, u32[]{:S(2)}) copy-start(f32[256,384]{0,1:T(8,128)} %copy-done.36) | copy-start | bytes 1179652
  460.7 9.9 %copy-start.41 = (f32[512,384]{0,1:T(8,128)S(1)}, f32[512,384]{0,1:T(8,128)}, u32[]{:S(2)}) copy-start(f32[512,384]{0,1:T(8,128)} %copy-done.39) | copy-start | bytes 2359300
  460.8 9.8 %copy-start.4 = (f32[1,1,1024,384]{2,3,1,0:T(8,128)S(1)}, f32[1,1,1024,384]{2,3,1,0:T(8,128)}, u32[]{:S(2)}) copy-start(f32[1,1,1024,384]{2,3,1,0:T(8,128)} %copy.18) | copy-start | bytes 4718596
  460.8 9.8 %copy-start.16 = (f32[512,384]{0,1:T(8,128)S(1)}, f32[512,384]{0,1:T(8,128)}, u32[]{:S(2)}) copy-start(f32[512,384]{0,1:T(8,128)} %copy-done.13) | copy-start | bytes 2359300
  471.9 15.2 %copy-start.6 = (f32[1024,384]{0,1:T(8,128)}, f32[1024,384]{0,1:T(8,128)S(1)}, u32[]{:S(2)}) copy-start(f32[1024,384]{0,1:T(8,128)S(1)} %bitcast_subtract_fusion) | copy-start | bytes 4718596
  471.9 11.1 %collective-permute-start.19 = (f32[256,384]{0,1:T(8,128)S(1)}, f32[256,384]{0,1:T(8,128)S(1)}, u32[]{:S(2)}, u32[]{:S(2)}) collective-permute-start(f32[256,384]{0,1:T(8,128)S(1)} %get-tuple-element.13), channel_id=1, source_target_pairs={{1,0},{2,1},{3,2},{4,3},{5,4},{6,5},{7,6},{9,8},{10,9},{11,10},{12... | collective-permute-start | bytes 1179656 | tf_op jit(solution)/shard_map/ppermute | solution.py:23
  483.0 4.1 copy-start.17
  483.0 4.1 copy-start.18
  483.0 4.1 copy-start.19
  484.1 11.4 %collective-permute-start.18 = (f32[256,384]{0,1:T(8,128)}, f32[256,384]{0,1:T(8,128)}, u32[]{:S(2)}, u32[]{:S(2)}) collective-permute-start(f32[256,384]{0,1:T(8,128)} %get-tuple-element.54), channel_id=1, source_target_pairs={{0,1},{1,2},{2,3},{3,4},{4,5},{5,6},{6,7},{8,9},{9,10},{10,11},{11... | collective-permute-start | bytes 1179656 | tf_op jit(solution)/shard_map/ppermute | solution.py:23
  491.8 5.2 %slice-start = ((f32[1024,384]{0,1:T(8,128)}), f32[512,384]{0,1:T(8,128)S(1)}, s32[]{:S(2)}) async-start(f32[1024,384]{0,1:T(8,128)} %copy-done.6), calls=%async_computation.4 | async-start | bytes 1572864 | tf_op jit(solution)/shard_map/slice | solution.py:62
  (5 other events, 5.4 us)
